TPU v7x, 32 devices: a whole 2x2x4 slice. The times are simulated.
32 devices in a mesh: dp: 32 (over z, y, x, core), rank: 1.
Axes of the slice: x: 2, y: 2, z: 4, core: 2. Of those that a mesh axis runs over, the one named last changes fastest.
Arguments:
- cloud_x: float32 [64, 65536], P(None, 'dp'), may hold values from -0.6 to 0.6
- cloud_y: float32 [64, 65536], P(None, 'dp'), may hold values from -0.6 to 0.6
- mass_x: float32 [65536], P('dp'), may hold values from 0.25 to 4
- mass_y: float32 [65536], P('dp'), may hold values from 0.25 to 4
- left_start: float32 [256, 65536], P('rank', 'dp'), may hold values from 0.25 to 204.8
- right_start: float32 [256, 65536], P('rank', 'dp'), may hold values from 0.25 to 204.8
- weight_start: float32 [256], P('rank'), may hold values from 0.25 to 4
Outputs:
- left_factor: float32 [256, 65536], P('rank', 'dp')
- right_factor: float32 [256, 65536], P('rank', 'dp')
- rank_weights: float32 [256], P('rank')
All inputs are finite; a program needn't handle non-finite values.
Results may differ from a plain program's by a relative error of at most 0.0003.
Values sent between devices are 32-bit elements; how exact they have to be, the bound alone decides.
A program may use at most 64 MiB of HBM per device.

v0:
```python
import jax
import jax.numpy as jnp
from jax import lax
from jax.sharding import PartitionSpec as P

RANK = 256
INNER = 4
MIRROR = 3


exact_mode = lax.Precision.HIGHEST
step_size = 2.0


def moments(cloud, factor):
    product = jnp.dot(cloud, factor.T, precision=exact_mode)
    square = jnp.dot(factor, jnp.sum(cloud * cloud, axis=0), precision=exact_mode)
    column = jnp.sum(factor, axis=1)
    return (product, square, column)


def widen(local_part, offset):
    shape_full = local_part.shape[:-1] + (RANK,)
    starts = (0,) * (local_part.ndim - 1) + (offset,)
    return lax.dynamic_update_slice(jnp.zeros(shape_full, jnp.float32), local_part, starts)


def narrow(full_part, offset, ranks_local):
    return lax.dynamic_slice_in_dim(full_part, offset, ranks_local, full_part.ndim - 1)


def shards(cloud_x, cloud_y, mass_x, mass_y, left_start, right_start, weight_start):
    ranks_local = left_start.shape[0]
    points_dev = left_start.shape[1]
    total_count = float(points_dev * lax.axis_size("dp"))
    offset = lax.axis_index("rank") * ranks_local
    mass_sums = lax.psum((jnp.sum(mass_x), jnp.sum(mass_y)), "dp")
    left_mass = mass_x * (total_count / mass_sums[0])
    right_mass = mass_y * (total_count / mass_sums[1])

    def project(kernel_left, kernel_right, kernel_weight):
        scale_left = jnp.ones((ranks_local,), jnp.float32)
        scale_right = jnp.ones((ranks_local,), jnp.float32)
        for repeat in range(INNER):
            row_left, row_right = lax.psum(
                (
                    jnp.dot(scale_left, kernel_left, precision=exact_mode),
                    jnp.dot(scale_right, kernel_right, precision=exact_mode),
                ),
                "rank",
            )
            point_left = left_mass / row_left
            point_right = right_mass / row_right
            column_left, column_right = lax.psum(
                (
                    jnp.dot(kernel_left, point_left, precision=exact_mode),
                    jnp.dot(kernel_right, point_right, precision=exact_mode),
                ),
                "dp",
            )
            weights = jnp.cbrt(
                kernel_weight * scale_left * column_left * scale_right * column_right
            )
            scale_left = weights / column_left
            scale_right = weights / column_right
        left = point_left[None, :] * kernel_left * scale_left[:, None]
        right = point_right[None, :] * kernel_right * scale_right[:, None]
        return (left, right, weights)

    left, right, weights = project(left_start, right_start, weight_start)
    for outer in range(MIRROR):
        prod_x, square_x, sums_q = moments(cloud_x, left)
        prod_y, square_y, sums_r = moments(cloud_y, right)
        root_weights = jnp.where(lax.axis_index("dp") == 0, weights, jnp.zeros_like(weights))
        full_px, full_py, full_sx, full_sy, full_q, full_r, full_w = lax.psum(
            (
                widen(prod_x, offset),
                widen(prod_y, offset),
                widen(square_x, offset),
                widen(square_y, offset),
                widen(sums_q, offset),
                widen(sums_r, offset),
                widen(root_weights, offset),
            ),
            ("dp", "rank"),
        )
        full_gq = full_sy / full_w
        full_gr = full_sx / full_w
        full_gg = -(
            full_sx * full_r + full_q * full_sy - 2.0 * jnp.sum(full_px * full_py, axis=0)
        ) / (full_w * full_w)
        mean_q = jnp.sum(full_gq) / RANK
        mean_r = jnp.sum(full_gr) / RANK
        mean_g = jnp.sum(full_gg) / RANK
        prod_x = narrow(full_px, offset, ranks_local)
        prod_y = narrow(full_py, offset, ranks_local)
        grad_q = narrow(full_gq, offset, ranks_local)
        grad_r = narrow(full_gr, offset, ranks_local)
        grad_g = narrow(full_gg, offset, ranks_local)
        field_q = (grad_q - mean_q)[:, None] - 2.0 * jnp.dot(
            prod_y.T, cloud_x, precision=exact_mode
        ) / weights[:, None]
        field_r = (grad_r - mean_r)[:, None] - 2.0 * jnp.dot(
            prod_x.T, cloud_y, precision=exact_mode
        ) / weights[:, None]
        kernel_left = left * jnp.exp(-step_size * field_q)
        kernel_right = right * jnp.exp(-step_size * field_r)
        kernel_weight = weights * jnp.exp(-step_size * (grad_g - mean_g))
        left, right, weights = project(kernel_left, kernel_right, kernel_weight)
    return (RANK * left, RANK * right, weights * (RANK / total_count))


def solution(mesh):
    in_specs = (
        P(None, "dp"),
        P(None, "dp"),
        P("dp"),
        P("dp"),
        P("rank", "dp"),
        P("rank", "dp"),
        P("rank"),
    )
    out_specs = (P("rank", "dp"), P("rank", "dp"), P("rank"))
    return jax.shard_map(shards, mesh=mesh, in_specs=in_specs, out_specs=out_specs, check_vma=False)
```

profile of v0, /device:TPU:0, one launch (start us, length us, event | category | flops | bytes accessed | tf_op | source)
XLA Modules:
  0.0 1324.1 jit_solution(662709427642656444)
XLA Ops:
  10.0 42.2 %all-reduce.19 = (f32[]{:T(128)}, f32[]{:T(128)}) all-reduce(f32[]{:T(128)} %reduce_sum.215, f32[]{:T(128)} %reduce_sum.214), channel_id=1, replica_groups=mesh['dp'=32,'rank'=1] {'dp'}, use_global_device_ids=true, to_apply=%region_4.0 | all-reduce | flops 2 | bytes 16 | tf_op jit(solution)/shard_map/psum | solution.py:37
  53.6 2.8 fusion.92
  61.0 40.5 %all-reduce.18 = (f32[256]{0:T(256)S(1)}, f32[256]{0:T(256)S(1)}) all-reduce(f32[256]{0:T(256)S(1)} %bitcast.402, f32[256]{0:T(256)S(1)} %bitcast.397), channel_id=1, replica_groups=mesh['dp'=32,'rank'=1] {'dp'}, use_global_device_ids=true, to_apply=%region_5.0 | all-reduce | flops 512 | bytes 4096 | tf_op jit(solution)/shard_map/psum | solution.py:54
  101.6 2.8 fusion.175
  109.0 39.8 %all-reduce.17 = (f32[256]{0:T(256)S(1)}, f32[256]{0:T(256)S(1)}) all-reduce(f32[256]{0:T(256)S(1)} %bitcast.389, f32[256]{0:T(256)S(1)} %bitcast.403), channel_id=1, replica_groups=mesh['dp'=32,'rank'=1] {'dp'}, use_global_device_ids=true, to_apply=%region_7.0 | all-reduce | flops 512 | bytes 4096 | tf_op jit(solution)/shard_map/psum | solution.py:54
  148.9 2.8 fusion.179
  156.3 40.6 %all-reduce.16 = (f32[256]{0:T(256)S(1)}, f32[256]{0:T(256)S(1)}) all-reduce(f32[256]{0:T(256)S(1)} %bitcast.390, f32[256]{0:T(256)S(1)} %bitcast.404), channel_id=1, replica_groups=mesh['dp'=32,'rank'=1] {'dp'}, use_global_device_ids=true, to_apply=%region_9.0 | all-reduce | flops 512 | bytes 4096 | tf_op jit(solution)/shard_map/psum | solution.py:54
  196.9 2.8 fusion.183
  204.3 39.9 %all-reduce.15 = (f32[256]{0:T(256)S(1)}, f32[256]{0:T(256)S(1)}) all-reduce(f32[256]{0:T(256)S(1)} %bitcast.388, f32[256]{0:T(256)S(1)} %bitcast.401), channel_id=1, replica_groups=mesh['dp'=32,'rank'=1] {'dp'}, use_global_device_ids=true, to_apply=%region_11.0 | all-reduce | flops 512 | bytes 4096 | tf_op jit(solution)/shard_map/psum | solution.py:54
  244.3 2.8 fusion.53
  247.0 2.8 fusion.52
  255.9 40.1 %all-reduce.14 = (f32[256]{0:T(256)S(1)}, f32[256]{0:T(256)S(1)}, f32[256]{0:T(256)S(1)}) all-reduce(f32[256]{0:T(256)S(1)} %bitcast.387, f32[256]{0:T(256)S(1)} %get-tuple-element.88, f32[256]{0:T(256)S(1)} %bitcast.386), channel_id=1, replica_groups=mesh['dp'=32,'rank'=1] {'dp','rank'}, use_global_device_ids=true, to_apply=%region_19.0 | all-reduce | flops 768 | bytes 6144 | tf_op jit(solution)/shard_map/psum | solution.py:75
  297.9 76.8 %all-reduce.31.cloned.1.call-done = (f32[64,256]{1,0:T(8,128)}, f32[64,256]{1,0:T(8,128)}) async-done(((f32[64,256]{1,0:T(8,128)}, f32[64,256]{1,0:T(8,128)}), (f32[64,256]{1,0:T(8,128)}, f32[64,256]{1,0:T(8,128)})) %all-reduce.31.cloned.1.call-update) | async-done | bytes 131088 | tf_op jit(solution)/shard_map/psum | solution.py:75
  375.5 3.2 fusion.4
  381.7 2.4 fusion.9
  386.9 39.7 %all-reduce.13 = (f32[256]{0:T(256)S(1)}, f32[256]{0:T(256)S(1)}, f32[256]{0:T(256)S(1)}, f32[256]{0:T(256)S(1)}) all-reduce(f32[256]{0:T(256)S(1)} %bitcast.417, f32[256]{0:T(256)S(1)} %get-tuple-element.122, f32[256]{0:T(256)S(1)} %get-tuple-element.123, f32[256]{0:T(256)S(1)} %bitcast.414), channel_id=1, replica_groups=mesh['dp'=32,'rank'=1] {'dp'}, use_global_device_ids=true, to_apply=%region_28.29 | all-reduce | flops 1024 | bytes 8192 | tf_op jit(solution)/shard_map/psum | solution.py:54
  427.9 2.8 fusion.189
  435.3 39.8 %all-reduce.12 = (f32[256]{0:T(256)S(1)}, f32[256]{0:T(256)S(1)}) all-reduce(f32[256]{0:T(256)S(1)} %bitcast.391, f32[256]{0:T(256)S(1)} %bitcast.405), channel_id=1, replica_groups=mesh['dp'=32,'rank'=1] {'dp'}, use_global_device_ids=true, to_apply=%region_30.31 | all-reduce | flops 512 | bytes 4096 | tf_op jit(solution)/shard_map/psum | solution.py:54
  475.2 2.8 fusion.193
  482.6 40.3 %all-reduce.11 = (f32[256]{0:T(256)S(1)}, f32[256]{0:T(256)S(1)}) all-reduce(f32[256]{0:T(256)S(1)} %bitcast.392, f32[256]{0:T(256)S(1)} %bitcast.406), channel_id=1, replica_groups=mesh['dp'=32,'rank'=1] {'dp'}, use_global_device_ids=true, to_apply=%region_32.33 | all-reduce | flops 512 | bytes 4096 | tf_op jit(solution)/shard_map/psum | solution.py:54
  522.9 2.8 fusion.197
  530.3 39.7 %all-reduce.10 = (f32[256]{0:T(256)S(1)}, f32[256]{0:T(256)S(1)}) all-reduce(f32[256]{0:T(256)S(1)} %bitcast.399, f32[256]{0:T(256)S(1)} %bitcast.411), channel_id=1, replica_groups=mesh['dp'=32,'rank'=1] {'dp'}, use_global_device_ids=true, to_apply=%region_34.35 | all-reduce | flops 512 | bytes 4096 | tf_op jit(solution)/shard_map/psum | solution.py:54
  570.1 3.5 fusion.40
  574.0 2.8 fusion.50
  578.6 2.8 fusion.51
  581.3 40.1 %all-reduce.9 = (f32[256]{0:T(256)S(1)}, f32[256]{0:T(256)S(1)}, f32[256]{0:T(256)S(1)}) all-reduce(f32[256]{0:T(256)S(1)} %bitcast.385, f32[256]{0:T(256)S(1)} %get-tuple-element.78, f32[256]{0:T(256)S(1)} %bitcast.383), channel_id=1, replica_groups=mesh['dp'=32,'rank'=1] {'dp','rank'}, use_global_device_ids=true, to_apply=%region_35.36 | all-reduce | flops 768 | bytes 6144 | tf_op jit(solution)/shard_map/psum | solution.py:75
  623.9 124.2 %all-reduce.29.cloned.1.call-done = (f32[64,256]{1,0:T(8,128)}, f32[64,256]{1,0:T(8,128)}) async-done(((f32[64,256]{1,0:T(8,128)}, f32[64,256]{1,0:T(8,128)}), (f32[64,256]{1,0:T(8,128)}, f32[64,256]{1,0:T(8,128)})) %all-reduce.29.cloned.1.call-update) | async-done | bytes 131088 | tf_op jit(solution)/shard_map/psum | solution.py:75
  748.1 4.1 fusion.14
  752.3 2.4 fusion.19
  760.4 39.6 %all-reduce.8 = (f32[256]{0:T(256)S(1)}, f32[256]{0:T(256)S(1)}, f32[256]{0:T(256)S(1)}, f32[256]{0:T(256)S(1)}) all-reduce(f32[256]{0:T(256)S(1)} %bitcast.415, f32[256]{0:T(256)S(1)} %fusion.37, f32[256]{0:T(256)S(1)} %fusion.41, f32[256]{0:T(256)S(1)} %bitcast.418), channel_id=1, replica_groups=mesh['dp'=32,'rank'=1] {'dp'}, use_global_device_ids=true, to_apply=%region_49.50 | all-reduce | flops 1024 | bytes 8192 | tf_op jit(solution)/shard_map/psum | solution.py:54
  801.4 2.8 fusion.203
  808.8 39.8 %all-reduce.7 = (f32[256]{0:T(256)S(1)}, f32[256]{0:T(256)S(1)}) all-reduce(f32[256]{0:T(256)S(1)} %bitcast.393, f32[256]{0:T(256)S(1)} %bitcast.407), channel_id=1, replica_groups=mesh['dp'=32,'rank'=1] {'dp'}, use_global_device_ids=true, to_apply=%region_51.52 | all-reduce | flops 512 | bytes 4096 | tf_op jit(solution)/shard_map/psum | solution.py:54
  848.6 2.8 fusion.207
  856.1 40.3 %all-reduce.6 = (f32[256]{0:T(256)S(1)}, f32[256]{0:T(256)S(1)}) all-reduce(f32[256]{0:T(256)S(1)} %bitcast.394, f32[256]{0:T(256)S(1)} %bitcast.408), channel_id=1, replica_groups=mesh['dp'=32,'rank'=1] {'dp'}, use_global_device_ids=true, to_apply=%region_53.54 | all-reduce | flops 512 | bytes 4096 | tf_op jit(solution)/shard_map/psum | solution.py:54
  896.3 2.8 fusion.211
  903.8 39.7 %all-reduce.5 = (f32[256]{0:T(256)S(1)}, f32[256]{0:T(256)S(1)}) all-reduce(f32[256]{0:T(256)S(1)} %bitcast.400, f32[256]{0:T(256)S(1)} %bitcast.412), channel_id=1, replica_groups=mesh['dp'=32,'rank'=1] {'dp'}, use_global_device_ids=true, to_apply=%region_55.56 | all-reduce | flops 512 | bytes 4096 | tf_op jit(solution)/shard_map/psum | solution.py:54
  945.7 2.8 fusion.49
  950.3 2.8 fusion.48
  953.0 40.4 %all-reduce.4 = (f32[256]{0:T(256)S(1)}, f32[256]{0:T(256)S(1)}, f32[256]{0:T(256)S(1)}) all-reduce(f32[256]{0:T(256)S(1)} %bitcast.384, f32[256]{0:T(256)S(1)} %get-tuple-element.68, f32[256]{0:T(256)S(1)} %bitcast.382), channel_id=1, replica_groups=mesh['dp'=32,'rank'=1] {'dp','rank'}, use_global_device_ids=true, to_apply=%region_61.62 | all-reduce | flops 768 | bytes 6144 | tf_op jit(solution)/shard_map/psum | solution.py:75
  997.3 122.9 %all-reduce.27.cloned.1.call-done = (f32[64,256]{1,0:T(8,128)}, f32[64,256]{1,0:T(8,128)}) async-done(((f32[64,256]{1,0:T(8,128)}, f32[64,256]{1,0:T(8,128)}), (f32[64,256]{1,0:T(8,128)}, f32[64,256]{1,0:T(8,128)})) %all-reduce.27.cloned.1.call-update) | async-done | bytes 131088 | tf_op jit(solution)/shard_map/psum | solution.py:75
  1120.2 4.0 fusion.29
  1124.3 2.4 fusion.24
  1132.4 39.6 %all-reduce.3 = (f32[256]{0:T(256)S(1)}, f32[256]{0:T(256)S(1)}, f32[256]{0:T(256)S(1)}, f32[256]{0:T(256)S(1)}) all-reduce(f32[256]{0:T(256)S(1)} %bitcast.419, f32[256]{0:T(256)S(1)} %fusion.43, f32[256]{0:T(256)S(1)} %fusion.47, f32[256]{0:T(256)S(1)} %bitcast.416), channel_id=1, replica_groups=mesh['dp'=32,'rank'=1] {'dp'}, use_global_device_ids=true, to_apply=%region_70.71 | all-reduce | flops 1024 | bytes 8192 | tf_op jit(solution)/shard_map/psum | solution.py:54
  1173.4 2.8 fusion.217
  1180.8 39.8 %all-reduce.2 = (f32[256]{0:T(256)S(1)}, f32[256]{0:T(256)S(1)}) all-reduce(f32[256]{0:T(256)S(1)} %bitcast.395, f32[256]{0:T(256)S(1)} %bitcast.409), channel_id=1, replica_groups=mesh['dp'=32,'rank'=1] {'dp'}, use_global_device_ids=true, to_apply=%region_72.73 | all-reduce | flops 512 | bytes 4096 | tf_op jit(solution)/shard_map/psum | solution.py:54
  1226.3 40.3 %all-reduce.1 = (f32[256]{0:T(256)S(1)}, f32[256]{0:T(256)S(1)}) all-reduce(f32[256]{0:T(256)S(1)} %bitcast.396, f32[256]{0:T(256)S(1)} %bitcast.410), channel_id=1, replica_groups=mesh['dp'=32,'rank'=1] {'dp'}, use_global_device_ids=true, to_apply=%region_74.75 | all-reduce | flops 512 | bytes 4096 | tf_op jit(solution)/shard_map/psum | solution.py:54
  1272.3 39.7 %all-reduce = (f32[256]{0:T(256)S(1)}, f32[256]{0:T(256)S(1)}) all-reduce(f32[256]{0:T(256)S(1)} %bitcast.398, f32[256]{0:T(256)S(1)} %bitcast.413), channel_id=1, replica_groups=mesh['dp'=32,'rank'=1] {'dp'}, use_global_device_ids=true, to_apply=%region_76.77 | all-reduce | flops 512 | bytes 4096 | tf_op jit(solution)/shard_map/psum | solution.py:54
  1312.7 3.2 multiply_multiply_fusion.1
  (217 shorter events, 103.7 us)
Async XLA Ops:
  7.2 49.3 %copy-start.30 = (f32[2048]{0:T(1024)S(1)}, f32[2048]{0:T(1024)}, u32[]{:S(2)}) copy-start(f32[2048]{0:T(1024)} %param.9) | copy-start | bytes 24580
  7.2 49.3 %copy-start = (f32[256,2048]{1,0:T(8,128)S(1)}, f32[256,2048]{1,0:T(8,128)}, u32[]{:S(2)}) copy-start(f32[256,2048]{1,0:T(8,128)} %param.11) | copy-start | bytes 6291460
  7.2 367.5 %all-reduce.31.cloned.1.call-start = ((), (), s32[]{:S(2)}) async-start(), calls=%async_computation.2 | async-start | bytes 262144 | tf_op jit(solution)/shard_map/psum | solution.py:75
  53.6 4.6 copy-start.1
  56.4 2.9 copy-start.29
  58.2 43.4 %copy-start.36 = (f32[256]{0:T(256)S(1)}, f32[256]{0:T(256)}, u32[]{:S(2)}) copy-start(f32[256]{0:T(256)} %param.13) | copy-start | bytes 3076
  101.6 2.9 copy-start.2
  148.9 2.9 copy-start.3
  196.9 2.9 copy-start.4
  201.5 42.8 %copy-start.28 = (f32[64,2048]{1,0:T(8,128)S(1)}, f32[64,2048]{1,0:T(8,128)}, u32[]{:S(2)}) copy-start(f32[64,2048]{1,0:T(8,128)} %param.7) | copy-start | bytes 1572868
  202.6 44.4 %copy-start.27 = (f32[64,2048]{1,0:T(8,128)S(1)}, f32[64,2048]{1,0:T(8,128)}, u32[]{:S(2)}) copy-start(f32[64,2048]{1,0:T(8,128)} %param.8) | copy-start | bytes 1572868
  244.2 2.8 copy-start.5
  249.8 498.3 %all-reduce.29.cloned.1.call-start = ((), (), s32[]{:S(2)}) async-start(), calls=%async_computation.1 | async-start | bytes 262144 | tf_op jit(solution)/shard_map/psum | solution.py:75
  252.3 1.8 copy-start.6
  378.8 2.9 copy-start.8
  378.8 2.9 copy-start.7
  378.8 2.9 copy-start.31
  384.1 2.8 copy-start.10
  427.8 2.9 copy-start.11
  427.9 4.6 copy-start.9
  475.2 2.9 copy-start.12
  522.9 2.9 copy-start.13
  570.1 3.6 copy-start.14
  623.3 496.9 %all-reduce.27.cloned.1.call-start = ((), (), s32[]{:S(2)}) async-start(), calls=%async_computation | async-start | bytes 262144 | tf_op jit(solution)/shard_map/psum | solution.py:75
  748.1 4.2 copy-start.32
  748.1 4.2 copy-start.34
  748.1 4.2 copy-start.15
  754.7 2.8 copy-start.16
  801.3 2.9 copy-start.17
  848.6 2.9 copy-start.18
  896.3 2.9 copy-start.19
  945.4 3.1 copy-start.20
  1120.2 4.1 copy-start.33
  1120.2 4.1 copy-start.35
  1124.2 6.4 copy-start.21
  1126.7 2.8 copy-start.23
  1132.4 43.8 %copy-start.22 = (f32[256,2048]{1,0:T(8,128)S(1)}, f32[256,2048]{1,0:T(8,128)}, u32[]{:S(2)}) copy-start(f32[256,2048]{1,0:T(8,128)} %copy-done.21) | copy-start | bytes 6291460
  1173.4 4.6 copy-start.24
  1220.6 2.8 copy-start.25
  1266.6 2.8 copy-start.26
Sparse Core Ops, SparseCore 0:
  249.9 124.6 all-reduce.30
  623.5 124.5 all-reduce.28
  995.5 124.6 all-reduce.26
where the time goes:
time: 1330 us; the launch traced here: 1320 us
  blocking collectives  802 us (60%)
  waiting for transfers between devices  324 us (24%)
  matrix products  157 us (12%)
  between operations  21.5 us (2%)
  other arithmetic  18.7 us (1%)
    psum x16, blocking collectives, project(): lax.psum((jnp.dot(kernel_left, point_left, precision=exact_mode), jnp.dot...  639 us
    psum x3, waiting for transfers between devices, shards(): lax.psum((widen(prod_x, offset), widen(prod_y, offset), widen(square_x, o...  324 us
    psum x3, blocking collectives, shards(): lax.psum((widen(prod_x, offset), widen(prod_y, offset), widen(square_x, o...  121 us
    psum x1, blocking collectives, shards(): mass_sums = lax.psum((jnp.sum(mass_x), jnp.sum(mass_y)), 'dp')  42.2 us
    dot_general x16, matrix products, project(): jnp.dot(scale_right, kernel_right, precision=exact_mode)  34.9 us
    dot_general x16, matrix products, project(): jnp.dot(kernel_left, point_left, precision=exact_mode)  27.7 us
    dot_general x16, matrix products, project(): jnp.dot(kernel_right, point_right, precision=exact_mode)  27.6 us
  transfers between devices with their start and end apart: 3, of which 3 were waited for; matrix products, arithmetic and copies ran while one was open for 1% of the time, Pallas kernels for 0%

commit v1 on v0

--- a/solution.py
+++ b/solution.py
@@ -1,6 +1,11 @@
+import functools
+import math
+
 import jax
 import jax.numpy as jnp
 from jax import lax
+from jax.experimental import pallas as pl
+from jax.experimental.pallas import tpu as pltpu
 from jax.sharding import PartitionSpec as P
 
 RANK = 256
@@ -110,6 +115,389 @@
     return (RANK * left, RANK * right, weights * (RANK / total_count))
 
 
+PLANE = 8
+LANE = 128
+AUG = 80
+LOG2E = math.log2(math.e)
+MESH = pl.DeviceIdType.MESH
+
+
+def split(x):
+    high = x.astype(jnp.bfloat16)
+    low = (x - high.astype(jnp.float32)).astype(jnp.bfloat16)
+    return high, low
+
+
+def cube_root(x):
+    y = jnp.exp(jnp.log(x) * (1.0 / 3.0))
+    y = y - (y - x / (y * y)) * (1.0 / 3.0)
+    return jnp.where(x > 0.0, y, x)
+
+
+def fused_kernel(
+    devices,
+    cx_ref, cy_ref, mx_ref, my_ref, ls_ref, rs_ref, ws_ref,
+    lo_ref, ro_ref, wo_ref,
+    kl, kr, vl, vr, ul, ur, pl_ref, pr_ref,
+    xh, xl, yh, yl, mom, weight_ref, sl_ref, sr_ref, coef_h, coef_l,
+    pay, got1, pay2, got2,
+    bpay, bgot1, bpay2, bgot2,
+    cgot1, cpay2, cgot2, full,
+    s_sem1, r_sem1, s_sem2, r_sem2, s_sem3, r_sem3, bs_sem1, br_sem1, bs_sem2, br_sem2,
+    cs_sem1, cr_sem1, cs_sem2, cr_sem2,
+):
+    ranks, points = ls_ref.shape
+    dims = cx_ref.shape[0]
+    total_count = float(points * devices)
+    planes = devices // PLANE
+    halves = ranks // LANE
+    tiles = points // LANE
+    blocks = ranks // 8
+    me = lax.axis_index("dp")
+    spot = lax.rem(me, PLANE)
+    level = lax.div(me, PLANE)
+
+    def in_plane(shift):
+        return level * PLANE + lax.rem(spot + shift, PLANE)
+
+    def across(shift):
+        return lax.rem(level + shift, planes) * PLANE + spot
+
+    barrier = pltpu.get_barrier_semaphore()
+    for shift in range(1, PLANE):
+        pl.semaphore_signal(barrier, inc=1, device_id={"dp": in_plane(shift)}, device_id_type=MESH)
+    for shift in range(1, planes):
+        pl.semaphore_signal(barrier, inc=1, device_id={"dp": across(shift)}, device_id_type=MESH)
+
+    def send(src, dst, s_sem, r_sem, target):
+        copy = pltpu.make_async_remote_copy(
+            src_ref=src, dst_ref=dst, send_sem=s_sem, recv_sem=r_sem,
+            device_id={"dp": target}, device_id_type=MESH,
+        )
+        copy.start()
+        return copy
+
+    def scatter_plane(src, got, s_sems, r_sems):
+        return [
+            send(src, got.at[spot], s_sems.at[shift], r_sems.at[shift], in_plane(shift))
+            for shift in range(1, PLANE)
+        ]
+
+    def scatter_across(src, got, s_sems, r_sems):
+        return [
+            send(src, got.at[level], s_sems.at[shift], r_sems.at[shift], across(shift))
+            for shift in range(1, planes)
+        ]
+
+    def finish(copies):
+        for copy in copies:
+            copy.wait_recv()
+        for copy in copies:
+            copy.wait_send()
+
+    def total_of(got, count):
+        acc = got[0]
+        for i in range(1, count):
+            acc = acc + got[i]
+        return acc
+
+    def reduce_all(value, parity, p1, g1, p2, g2, ss1, rs1, ss2, rs2):
+        src = p1.at[parity]
+        src[...] = value
+        g1.at[parity][spot] = value
+        finish(scatter_plane(src, g1.at[parity], ss1.at[parity], rs1.at[parity]))
+        part = total_of(g1.at[parity], PLANE)
+        src2 = p2.at[parity]
+        src2[...] = part
+        g2.at[parity][level] = part
+        finish(scatter_across(src2, g2.at[parity], ss2.at[parity], rs2.at[parity]))
+        return total_of(g2.at[parity], planes)
+
+    def small_reduce(value, parity):
+        return reduce_all(value, parity, pay, got1, pay2, got2, s_sem1, r_sem1, s_sem2, r_sem2)
+
+    def spread(dst, value):
+        for h in range(halves):
+            square = jnp.broadcast_to(value[h : h + 1, :], (LANE, LANE))
+            dst[h * LANE : (h + 1) * LANE, :] = square.T
+
+    def row_of(b):
+        return pl.ds(pl.multiple_of(b * 8, 8), 8)
+
+    def rows_pass():
+        def body(b, acc):
+            al, ar = acc
+            rows = row_of(b)
+            al = al + kl[rows, :] * jnp.concatenate([vl[rows, :]] * tiles, axis=1)
+            ar = ar + kr[rows, :] * jnp.concatenate([vr[rows, :]] * tiles, axis=1)
+            return al, ar
+
+        zero = jnp.zeros((8, points), jnp.float32)
+        al, ar = lax.fori_loop(0, blocks, body, (zero, zero), unroll=4)
+        ul[...] = jnp.broadcast_to(sl_ref[...] / jnp.sum(al, axis=0, keepdims=True), (8, points))
+        ur[...] = jnp.broadcast_to(sr_ref[...] / jnp.sum(ar, axis=0, keepdims=True), (8, points))
+
+    def columns_pass():
+        bl, br = ul[...], ur[...]
+
+        def fold(x):
+            parts = [x[:, i * LANE : (i + 1) * LANE] for i in range(tiles)]
+            while len(parts) > 1:
+                parts = [parts[i] + parts[i + 1] for i in range(0, len(parts) - 1, 2)] + (
+                    parts[-1:] if len(parts) % 2 else []
+                )
+            return parts[0]
+
+        def body(b, carry):
+            rows = row_of(b)
+            pl_ref[rows, :] = fold(kl[rows, :] * bl)
+            pr_ref[rows, :] = fold(kr[rows, :] * br)
+            return carry
+
+        lax.fori_loop(0, blocks, body, 0, unroll=4)
+        out = []
+        for ref in (pl_ref, pr_ref):
+            for h in range(halves):
+                out.append(jnp.sum(ref[h * LANE : (h + 1) * LANE, :].T, axis=0, keepdims=True))
+        return jnp.concatenate(out, axis=0)
+
+    def rescale(cl, cr, v1, v2):
+        g = cube_root(weight_ref[...] * v1 * cl * v2 * cr)
+        v1, v2 = g / cl, g / cr
+        spread(vl, v1)
+        spread(vr, v2)
+        return g, v1, v2
+
+    def small_step(parity, v1, v2):
+        rows_pass()
+        sums = small_reduce(columns_pass(), parity)
+        return rescale(sums[:halves], sums[halves : 2 * halves], v1, v2)
+
+    for src, high, low in ((cx_ref, xh, xl), (cy_ref, yh, yl)):
+        cloud = src[...]
+        square = jnp.sum(cloud * cloud, axis=0, keepdims=True)
+        place = lax.broadcasted_iota(jnp.int32, (LANE - dims, points), 0)
+        extra = jnp.where(place == 0, square, jnp.where(place == 1, 1.0, 0.0))
+        high[:dims, :], low[:dims, :] = split(cloud)
+        high[dims:, :], low[dims:, :] = split(extra)
+    ones = jnp.ones((halves, LANE), jnp.float32)
+    weight_ref[...] = ws_ref[...]
+    vl[...] = jnp.ones((ranks, LANE), jnp.float32)
+    vr[...] = jnp.ones((ranks, LANE), jnp.float32)
+    sl_ref[...] = mx_ref[...]
+    sr_ref[...] = my_ref[...]
+    kl[...] = ls_ref[...]
+    kr[...] = rs_ref[...]
+    rows_pass()
+    first = columns_pass()
+    pl.semaphore_wait(barrier, PLANE - 1 + planes - 1)
+
+    sums = small_reduce(first, 0)
+    cl, cr = sums[:halves], sums[halves : 2 * halves]
+    al = total_count / jnp.sum(cl)
+    ar = total_count / jnp.sum(cr)
+    sl_ref[...] = sl_ref[...] * al
+    sr_ref[...] = sr_ref[...] * ar
+    g, v1, v2 = rescale(cl * al, cr * ar, ones, ones)
+
+    def inner(i, carry):
+        _, v1, v2 = carry
+        return small_step(lax.rem(i, 2), v1, v2)
+
+    _, v1, v2 = lax.fori_loop(1, INNER - 1, inner, (g, v1, v2))
+
+    chunk = 2 * LANE
+
+    def moment_pass(k_ref, u_ref, high, low):
+        acc = jnp.zeros((AUG, ranks), jnp.float32)
+        nt = (((1,), (1,)), ((), ()))
+        for c in range(points // chunk):
+            cols = slice(c * chunk, (c + 1) * chunk)
+            w = k_ref[:, cols] * u_ref[0:1, cols]
+            wh, wl = split(w)
+            h, l = high[:AUG, cols], low[:AUG, cols]
+            acc = acc + lax.dot_general(h, wh, nt, preferred_element_type=jnp.float32)
+            acc = acc + lax.dot_general(h, wl, nt, preferred_element_type=jnp.float32)
+            acc = acc + lax.dot_general(l, wh, nt, preferred_element_type=jnp.float32)
+        return acc
+
+    def lanes(row):
+        return [row[:, h * LANE : (h + 1) * LANE] for h in range(halves)]
+
+    def wide(value):
+        return jnp.concatenate([value[h : h + 1, :] for h in range(halves)], axis=1)
+
+    def update(k_ref, u_ref, v_ref, high, low):
+        for c in range(points // chunk):
+            cols = slice(c * chunk, (c + 1) * chunk)
+            h, l = high[:, cols], low[:, cols]
+            a, b = coef_h[...], coef_l[...]
+            e = jnp.dot(a, h, preferred_element_type=jnp.float32)
+            e = e + jnp.dot(a, l, preferred_element_type=jnp.float32)
+            e = e + jnp.dot(b, h, preferred_element_type=jnp.float32)
+            scale = jnp.concatenate([v_ref[...]] * (chunk // LANE), axis=1)
+            k_ref[:, cols] = k_ref[:, cols] * u_ref[0:1, cols] * scale * jnp.exp2(e)
+
+    per = dims // PLANE
+
+    def coefficients(centre, moment):
+        mean = jnp.sum(moment) / ranks
+        bias = (-2.0 * LOG2E) * (moment - mean)
+        place = lax.broadcasted_iota(jnp.int32, (LANE - dims, ranks), 0)
+        extra = jnp.where(place == 1, bias, 0.0)
+        full_rows = jnp.concatenate([centre * (4.0 * LOG2E), extra], axis=0)
+        high, low = split(full_rows.T)
+        coef_h[...] = high
+        coef_l[...] = low
+
+    def outer_step(outer, carry):
+        v1, v2 = carry
+        rows_pass()
+        mom_x = moment_pass(kl, ul, xh, xl)
+        mom_y = moment_pass(kr, ur, yh, yl)
+        for j in range(PLANE):
+            mom[j, 0] = mom_x[j * per : (j + 1) * per]
+            mom[j, 1] = mom_y[j * per : (j + 1) * per]
+        copies = []
+        for shift in range(1, PLANE):
+            target = lax.rem(spot + shift, PLANE)
+            copies.append(
+                send(mom.at[target], cgot1.at[spot], cs_sem1.at[shift], cr_sem1.at[shift], in_plane(shift))
+            )
+        cgot1[spot] = mom[spot]
+        value = jnp.concatenate(
+            lanes(mom_x[dims + 1 : dims + 2]) + lanes(mom_y[dims + 1 : dims + 2])
+            + lanes(mom_x[dims : dims + 1]) + lanes(mom_y[dims : dims + 1]),
+            axis=0,
+        )
+        bpay[...] = value
+        bgot1[spot] = value
+        small = scatter_plane(bpay, bgot1, bs_sem1, br_sem1)
+        finish(small)
+        part = total_of(bgot1, PLANE)
+        bpay2[...] = part
+        bgot2[level] = part
+        small = scatter_across(bpay2, bgot2, bs_sem2, br_sem2)
+        finish(copies)
+        part = total_of(cgot1, PLANE)
+        cpay2[...] = part
+        cgot2[level] = part
+        copies = scatter_across(cpay2, cgot2, cs_sem2, cr_sem2)
+        finish(small)
+        sums = total_of(bgot2, planes)
+        cl, cr = sums[:halves], sums[halves : 2 * halves]
+        sx = wide(sums[2 * halves : 3 * halves] / cl)
+        sy = wide(sums[3 * halves : 4 * halves] / cr)
+        g, v1, v2 = rescale(cl, cr, v1, v2)
+        finish(copies)
+        full[spot] = total_of(cgot2, planes)
+        finish(
+            [
+                send(full.at[spot], full.at[spot], s_sem3.at[shift], r_sem3.at[shift], in_plane(shift))
+                for shift in range(1, PLANE)
+            ]
+        )
+        inv_l, inv_r = wide(1.0 / cl), wide(1.0 / cr)
+        centre_x = jnp.concatenate([full[j, 0] for j in range(PLANE)], axis=0) * inv_l
+        centre_y = jnp.concatenate([full[j, 1] for j in range(PLANE)], axis=0) * inv_r
+        coefficients(centre_y, sy)
+        update(kl, ul, vl, xh, xl)
+        coefficients(centre_x, sx)
+        update(kr, ur, vr, yh, yl)
+        gg = -(sx + sy - 2.0 * jnp.sum(centre_x * centre_y, axis=0, keepdims=True))
+        tilt = jnp.exp(-step_size * (gg - jnp.sum(gg) / ranks))
+        weight_ref[...] = g * jnp.concatenate(lanes(tilt), axis=0)
+        vl[...] = jnp.ones((ranks, LANE), jnp.float32)
+        vr[...] = jnp.ones((ranks, LANE), jnp.float32)
+        carry = (g, ones, ones)
+        steps = jnp.where(outer == MIRROR - 1, INNER, INNER - 1)
+
+        def again(i, carry):
+            return small_step(lax.rem(i + 1, 2), carry[1], carry[2])
+
+        g, v1, v2 = lax.fori_loop(0, steps, again, carry)
+        wo_ref[...] = g * (ranks / total_count)
+        return v1, v2
+
+    lax.fori_loop(0, MIRROR, outer_step, (v1, v2))
+
+    def emit(b, carry):
+        rows = row_of(b)
+        sl = jnp.concatenate([vl[rows, :]] * tiles, axis=1)
+        sr = jnp.concatenate([vr[rows, :]] * tiles, axis=1)
+        lo_ref[rows, :] = kl[rows, :] * ul[...] * sl * float(ranks)
+        ro_ref[rows, :] = kr[rows, :] * ur[...] * sr * float(ranks)
+        return carry
+
+    lax.fori_loop(0, blocks, emit, 0)
+
+
+def fused(cloud_x, cloud_y, mass_x, mass_y, left_start, right_start, weight_start):
+    devices = lax.axis_size("dp")
+    ranks, points = left_start.shape
+    dims = cloud_x.shape[0]
+    planes = devices // PLANE
+    halves = ranks // LANE
+    per = dims // PLANE
+    f32 = jnp.float32
+    dma = pltpu.SemaphoreType.DMA
+    vmem = pl.BlockSpec(memory_space=pltpu.VMEM)
+    left, right, weights = pl.pallas_call(
+        functools.partial(fused_kernel, devices),
+        out_shape=(
+            jax.ShapeDtypeStruct((ranks, points), f32),
+            jax.ShapeDtypeStruct((ranks, points), f32),
+            jax.ShapeDtypeStruct((halves, LANE), f32),
+        ),
+        in_specs=[vmem] * 7,
+        out_specs=(vmem,) * 3,
+        scratch_shapes=[
+            pltpu.VMEM((ranks, points), f32),
+            pltpu.VMEM((ranks, points), f32),
+            pltpu.VMEM((ranks, LANE), f32),
+            pltpu.VMEM((ranks, LANE), f32),
+            pltpu.VMEM((8, points), f32),
+            pltpu.VMEM((8, points), f32),
+            pltpu.VMEM((ranks, LANE), f32),
+            pltpu.VMEM((ranks, LANE), f32),
+            pltpu.VMEM((LANE, points), jnp.bfloat16),
+            pltpu.VMEM((LANE, points), jnp.bfloat16),
+            pltpu.VMEM((LANE, points), jnp.bfloat16),
+            pltpu.VMEM((LANE, points), jnp.bfloat16),
+            pltpu.VMEM((PLANE, 2, per, ranks), f32),
+            pltpu.VMEM((halves, LANE), f32),
+            pltpu.VMEM((1, points), f32),
+            pltpu.VMEM((1, points), f32),
+            pltpu.VMEM((ranks, LANE), jnp.bfloat16),
+            pltpu.VMEM((ranks, LANE), jnp.bfloat16),
+            pltpu.VMEM((2, 2 * halves, LANE), f32),
+            pltpu.VMEM((2, PLANE, 2 * halves, LANE), f32),
+            pltpu.VMEM((2, 2 * halves, LANE), f32),
+            pltpu.VMEM((2, planes, 2 * halves, LANE), f32),
+            pltpu.VMEM((4 * halves, LANE), f32),
+            pltpu.VMEM((PLANE, 4 * halves, LANE), f32),
+            pltpu.VMEM((4 * halves, LANE), f32),
+            pltpu.VMEM((planes, 4 * halves, LANE), f32),
+            pltpu.VMEM((PLANE, 2, per, ranks), f32),
+            pltpu.VMEM((2, per, ranks), f32),
+            pltpu.VMEM((planes, 2, per, ranks), f32),
+            pltpu.VMEM((PLANE, 2, per, ranks), f32),
+            dma((2, PLANE)), dma((2, PLANE)), dma((2, planes)), dma((2, planes)),
+            dma((PLANE,)), dma((PLANE,)),
+            dma((PLANE,)), dma((PLANE,)), dma((planes,)), dma((planes,)),
+            dma((PLANE,)), dma((PLANE,)), dma((planes,)), dma((planes,)),
+        ],
+        compiler_params=pltpu.CompilerParams(
+            collective_id=0, has_side_effects=True, vmem_limit_bytes=48 * 1024 * 1024
+        ),
+        name="sinkhorn",
+    )(
+        cloud_x, cloud_y, mass_x.reshape(1, points), mass_y.reshape(1, points),
+        left_start, right_start, weight_start.reshape(halves, LANE),
+    )
+    return left, right, weights.reshape(ranks)
+
+
 def solution(mesh):
     in_specs = (
         P(None, "dp"),
@@ -121,4 +509,8 @@
         P("rank"),
     )
     out_specs = (P("rank", "dp"), P("rank", "dp"), P("rank"))
-    return jax.shard_map(shards, mesh=mesh, in_specs=in_specs, out_specs=out_specs, check_vma=False)
+    if mesh.shape["rank"] == 1 and mesh.shape["dp"] % PLANE == 0:
+        body = fused
+    else:
+        body = shards
+    return jax.shard_map(body, mesh=mesh, in_specs=in_specs, out_specs=out_specs, check_vma=False)

time: 1330 us -> 162 us (0.12)
  blocking collectives: 802 us -> 0 us
  waiting for transfers between devices: 324 us -> 0 us
  matrix products: 157 us -> 0 us
  Pallas kernels: 0 us -> 154 us
  between operations: 21.5 us -> 0.65 us
  other arithmetic: 18.7 us -> 0 us
    psum x20 -> x0, blocking collectives: 802 us -> none  [the longest x16 639 us: project(): lax.psum((jnp.dot(kernel_left, point_left, precision=exact_mode), jnp.dot...]
    psum x3 -> x0, waiting for transfers between devices: 324 us -> none  [shards(): lax.psum((widen(prod_x, offset), widen(prod_y, offset), widen(square_x, o...]
    dot_general x82 -> x0, matrix products: 157 us -> none  [the longest x16 34.9 us: project(): jnp.dot(scale_right, kernel_right, precision=exact_mode)]
    pallas_call x0 -> x1, Pallas kernels: none -> 154 us  [fused(): pl.pallas_call(functools.partial(fused_kernel, devices), out_shape=(jax.S...]
  transfers between devices with their start and end apart: 3 -> 0, of which waited for: 3 -> 0; matrix products, arithmetic and copies ran while one was open for 1% -> 0% of each run, Pallas kernels for 0% -> 0%
where the time goes in v1:
time: 162 us
  Pallas kernels  154 us (95%)
  local copies, waits for them, and re-layouts  7.35 us (5%)
    pallas_call x1, Pallas kernels, fused(): pl.pallas_call(functools.partial(fused_kernel, devices), out_shape=(jax.S...  154 us
    unnamed x13, local copies, waits for them, and re-layouts  7.35 us

profile of v1, /device:TPU:0, one launch (start us, length us, event | category | flops | bytes accessed | tf_op | source)
XLA Modules:
  0.0 162.1 jit_solution(14156737904168404136)
XLA Ops:
  0.6 0.0 copy-start
  0.6 1.0 copy-done
  1.7 0.0 copy-start.1
  1.7 1.0 copy-done.1
  2.7 0.0 copy-start.2
  2.7 0.7 copy-done.2
  3.4 0.0 copy-start.3
  3.4 0.7 copy-done.3
  4.1 0.0 copy-start.4
  4.1 0.7 copy-done.4
  4.8 154.1 %sinkhorn.1 = (f32[256,2048]{1,0:T(8,128)S(1)}, f32[256,2048]{1,0:T(8,128)S(1)}, f32[2,128]{1,0:T(2,128)S(1)}) custom-call(f32[64,2048]{1,0:T(8,128)S(1)} %copy-done, f32[64,2048]{1,0:T(8,128)S(1)} %copy-done.1, f32[1,2048]{1,0:T(1,128)S(1)} %bitcast.4, f32[1,2048]{1,0:T(1,128)S(1)} %bitcast.5, f32[256,2048]{1,0:T(8,128)} %ls_ref.1, f32[256,2048]{1,0:T(8,128)} %rs_ref.1, ...), custom_call_target="tpu_custom_call" | custom-call | tf_op jit(solution)/shard_map/sinkhorn/pallas_call | solution.py:445
  158.9 1.3 copy.13
  160.2 1.3 copy.14
  161.5 0.6 copy.15
Async XLA Ops:
  0.6 1.0 copy-start
  1.7 1.0 copy-start.1
  2.7 0.7 copy-start.2
  3.4 0.7 copy-start.3
  4.1 0.7 copy-start.4

commit v2 on v1

--- a/solution.py
+++ b/solution.py
@@ -137,14 +137,13 @@
 def fused_kernel(
     devices,
     cx_ref, cy_ref, mx_ref, my_ref, ls_ref, rs_ref, ws_ref,
-    lo_ref, ro_ref, wo_ref,
-    kl, kr, vl, vr, ul, ur, pl_ref, pr_ref,
+    kl, kr, wo_ref,
+    vl, vr, ul, ur, pl_ref, pr_ref,
     xh, xl, yh, yl, mom, weight_ref, sl_ref, sr_ref, coef_h, coef_l,
-    pay, got1, pay2, got2,
-    bpay, bgot1, bpay2, bgot2,
+    pay, got1, bpay, bgot1,
     cgot1, cpay2, cgot2, full,
-    s_sem1, r_sem1, s_sem2, r_sem2, s_sem3, r_sem3, bs_sem1, br_sem1, bs_sem2, br_sem2,
-    cs_sem1, cr_sem1, cs_sem2, cr_sem2,
+    s_sem1, r_sem1, s_sem3, r_sem3, bs_sem1, br_sem1,
+    cs_sem1, cr_sem1, cs_sem2, cr_sem2, in_sem,
 ):
     ranks, points = ls_ref.shape
     dims = cx_ref.shape[0]
@@ -163,11 +162,15 @@
     def across(shift):
         return lax.rem(level + shift, planes) * PLANE + spot
 
+    loads = [
+        pltpu.make_async_copy(src, dst, in_sem.at[i])
+        for i, (src, dst) in enumerate(((ls_ref, kl), (rs_ref, kr)))
+    ]
+    for load in loads:
+        load.start()
     barrier = pltpu.get_barrier_semaphore()
-    for shift in range(1, PLANE):
-        pl.semaphore_signal(barrier, inc=1, device_id={"dp": in_plane(shift)}, device_id_type=MESH)
-    for shift in range(1, planes):
-        pl.semaphore_signal(barrier, inc=1, device_id={"dp": across(shift)}, device_id_type=MESH)
+    for shift in range(1, devices):
+        pl.semaphore_signal(barrier, inc=1, device_id={"dp": lax.rem(me + shift, devices)}, device_id_type=MESH)
 
     def send(src, dst, s_sem, r_sem, target):
         copy = pltpu.make_async_remote_copy(
@@ -177,12 +180,6 @@
         copy.start()
         return copy
 
-    def scatter_plane(src, got, s_sems, r_sems):
-        return [
-            send(src, got.at[spot], s_sems.at[shift], r_sems.at[shift], in_plane(shift))
-            for shift in range(1, PLANE)
-        ]
-
     def scatter_across(src, got, s_sems, r_sems):
         return [
             send(src, got.at[level], s_sems.at[shift], r_sems.at[shift], across(shift))
@@ -201,20 +198,30 @@
             acc = acc + got[i]
         return acc
 
-    def reduce_all(value, parity, p1, g1, p2, g2, ss1, rs1, ss2, rs2):
-        src = p1.at[parity]
+    def exchange_all(src, got, s_sems, r_sems):
+        copies = []
+        for climb in range(planes):
+            for shift in range(PLANE):
+                step = climb * PLANE + shift
+                if step == 0:
+                    continue
+                target = lax.rem(level + climb, planes) * PLANE + lax.rem(spot + shift, PLANE)
+                copies.append(send(src, got.at[me], s_sems.at[step], r_sems.at[step], target))
+        return copies
+
+    def tree(got):
+        parts = [got[i] for i in range(devices)]
+        while len(parts) > 1:
+            pairs = [parts[i] + parts[i + 1] for i in range(0, len(parts) - 1, 2)]
+            parts = pairs + ([parts[-1]] if len(parts) % 2 else [])
+        return parts[0]
+
+    def small_reduce(value, parity):
+        src, got = pay.at[parity], got1.at[parity]
         src[...] = value
-        g1.at[parity][spot] = value
-        finish(scatter_plane(src, g1.at[parity], ss1.at[parity], rs1.at[parity]))
-        part = total_of(g1.at[parity], PLANE)
-        src2 = p2.at[parity]
-        src2[...] = part
-        g2.at[parity][level] = part
-        finish(scatter_across(src2, g2.at[parity], ss2.at[parity], rs2.at[parity]))
-        return total_of(g2.at[parity], planes)
-
-    def small_reduce(value, parity):
-        return reduce_all(value, parity, pay, got1, pay2, got2, s_sem1, r_sem1, s_sem2, r_sem2)
+        got[me] = value
+        finish(exchange_all(src, got, s_sem1.at[parity], r_sem1.at[parity]))
+        return tree(got)
 
     def spread(dst, value):
         for h in range(halves):
@@ -286,11 +293,11 @@
     vr[...] = jnp.ones((ranks, LANE), jnp.float32)
     sl_ref[...] = mx_ref[...]
     sr_ref[...] = my_ref[...]
-    kl[...] = ls_ref[...]
-    kr[...] = rs_ref[...]
+    for load in loads:
+        load.wait()
     rows_pass()
     first = columns_pass()
-    pl.semaphore_wait(barrier, PLANE - 1 + planes - 1)
+    pl.semaphore_wait(barrier, devices - 1)
 
     sums = small_reduce(first, 0)
     cl, cr = sums[:halves], sums[halves : 2 * halves]
@@ -371,20 +378,15 @@
             axis=0,
         )
         bpay[...] = value
-        bgot1[spot] = value
-        small = scatter_plane(bpay, bgot1, bs_sem1, br_sem1)
-        finish(small)
-        part = total_of(bgot1, PLANE)
-        bpay2[...] = part
-        bgot2[level] = part
-        small = scatter_across(bpay2, bgot2, bs_sem2, br_sem2)
+        bgot1[me] = value
+        small = exchange_all(bpay, bgot1, bs_sem1, br_sem1)
         finish(copies)
         part = total_of(cgot1, PLANE)
         cpay2[...] = part
         cgot2[level] = part
         copies = scatter_across(cpay2, cgot2, cs_sem2, cr_sem2)
         finish(small)
-        sums = total_of(bgot2, planes)
+        sums = tree(bgot1)
         cl, cr = sums[:halves], sums[halves : 2 * halves]
         sx = wide(sums[2 * halves : 3 * halves] / cl)
         sy = wide(sums[3 * halves : 4 * halves] / cr)
@@ -425,8 +427,8 @@
         rows = row_of(b)
         sl = jnp.concatenate([vl[rows, :]] * tiles, axis=1)
         sr = jnp.concatenate([vr[rows, :]] * tiles, axis=1)
-        lo_ref[rows, :] = kl[rows, :] * ul[...] * sl * float(ranks)
-        ro_ref[rows, :] = kr[rows, :] * ur[...] * sr * float(ranks)
+        kl[rows, :] = kl[rows, :] * ul[...] * sl * float(ranks)
+        kr[rows, :] = kr[rows, :] * ur[...] * sr * float(ranks)
         return carry
 
     lax.fori_loop(0, blocks, emit, 0)
@@ -449,11 +451,9 @@
             jax.ShapeDtypeStruct((ranks, points), f32),
             jax.ShapeDtypeStruct((halves, LANE), f32),
         ),
-        in_specs=[vmem] * 7,
+        in_specs=[vmem] * 4 + [pl.BlockSpec(memory_space=pl.ANY)] * 2 + [vmem],
         out_specs=(vmem,) * 3,
         scratch_shapes=[
-            pltpu.VMEM((ranks, points), f32),
-            pltpu.VMEM((ranks, points), f32),
             pltpu.VMEM((ranks, LANE), f32),
             pltpu.VMEM((ranks, LANE), f32),
             pltpu.VMEM((8, points), f32),
@@ -471,24 +471,18 @@
             pltpu.VMEM((ranks, LANE), jnp.bfloat16),
             pltpu.VMEM((ranks, LANE), jnp.bfloat16),
             pltpu.VMEM((2, 2 * halves, LANE), f32),
-            pltpu.VMEM((2, PLANE, 2 * halves, LANE), f32),
-            pltpu.VMEM((2, 2 * halves, LANE), f32),
-            pltpu.VMEM((2, planes, 2 * halves, LANE), f32),
+            pltpu.VMEM((2, devices, 2 * halves, LANE), f32),
             pltpu.VMEM((4 * halves, LANE), f32),
-            pltpu.VMEM((PLANE, 4 * halves, LANE), f32),
-            pltpu.VMEM((4 * halves, LANE), f32),
-            pltpu.VMEM((planes, 4 * halves, LANE), f32),
+            pltpu.VMEM((devices, 4 * halves, LANE), f32),
             pltpu.VMEM((PLANE, 2, per, ranks), f32),
             pltpu.VMEM((2, per, ranks), f32),
             pltpu.VMEM((planes, 2, per, ranks), f32),
             pltpu.VMEM((PLANE, 2, per, ranks), f32),
-            dma((2, PLANE)), dma((2, PLANE)), dma((2, planes)), dma((2, planes)),
-            dma((PLANE,)), dma((PLANE,)),
-            dma((PLANE,)), dma((PLANE,)), dma((planes,)), dma((planes,)),
-            dma((PLANE,)), dma((PLANE,)), dma((planes,)), dma((planes,)),
+            dma((2, devices)), dma((2, devices)), dma((PLANE,)), dma((PLANE,)), dma((devices,)), dma((devices,)),
+            dma((PLANE,)), dma((PLANE,)), dma((planes,)), dma((planes,)), dma((2,)),
         ],
         compiler_params=pltpu.CompilerParams(
-            collective_id=0, has_side_effects=True, vmem_limit_bytes=48 * 1024 * 1024
+            collective_id=0, has_side_effects=True, vmem_limit_bytes=63 * 1024 * 1024
         ),
         name="sinkhorn",
     )(

time: 162 us -> 142 us (0.88)
  Pallas kernels: 154 us -> 136 us
  local copies, waits for them, and re-layouts: 7.35 us -> 5.17 us
    pallas_call x1, Pallas kernels: 154 us -> 136 us  [fused(): pl.pallas_call(functools.partial(fused_kernel, devices), out_shape=(jax.S...]
    unnamed x13 -> x7, local copies, waits for them, and re-layouts: 7.35 us -> 5.17 us
where the time goes in v2:
time: 142 us; the launch traced here: 141 us
  Pallas kernels  136 us (96%)
  local copies, waits for them, and re-layouts  5.17 us (4%)
    pallas_call x1, Pallas kernels, fused(): pl.pallas_call(functools.partial(fused_kernel, devices), out_shape=(jax.S...  136 us
    unnamed x7, local copies, waits for them, and re-layouts  5.17 us

profile of v2, /device:TPU:0, one launch (start us, length us, event | category | flops | bytes accessed | tf_op | source)
XLA Modules:
  0.0 141.4 jit_solution(1590143417386512766)
XLA Ops:
  0.6 135.5 %sinkhorn.1 = (f32[256,2048]{1,0:T(8,128)}, f32[256,2048]{1,0:T(8,128)}, f32[2,128]{1,0:T(2,128)}) custom-call(f32[64,2048]{1,0:T(8,128)} %cx_ref.1, f32[64,2048]{1,0:T(8,128)} %cy_ref.1, f32[1,2048]{1,0:T(1,128)} %bitcast.4, f32[1,2048]{1,0:T(1,128)} %bitcast.5, f32[256,2048]{1,0:T(8,128)} %ls_ref.1, f32[256,2048]{1,0:T(8,128)} %rs_ref.1, f32[2,128]{1,0:T(2,128)} %bitcast.7), custom_call_target="tpu_custom_call" | custom-call | tf_op jit(solution)/shard_map/sinkhorn/pallas_call | solution.py:447
  136.2 0.0 copy-start
  136.2 3.3 %copy.13 = f32[256,2048]{1,0:T(8,128)} copy(f32[256,2048]{1,0:T(8,128)} %get-tuple-element.12) | data formatting | bytes 4194304
  139.5 0.0 copy-done
  139.5 0.0 copy-start.1
  139.5 1.3 copy.14
  140.8 0.0 copy-done.1
  140.8 0.6 copy.15
Async XLA Ops:
  136.2 3.3 %copy-start = (f32[256,2048]{1,0:T(8,128)S(1)}, f32[256,2048]{1,0:T(8,128)}, u32[]{:S(2)}) copy-start(f32[256,2048]{1,0:T(8,128)} %get-tuple-element.13) | copy-start | bytes 6291460
  139.5 1.3 copy-start.1
